TPU v7x, 512 devices: a whole 4x4x16 slice. The times are simulated.
512 devices in a mesh: row: 32 (over z, core), vec: 16 (over y, x).
Axes of the slice: x: 4, y: 4, z: 16, core: 2. Of those that a mesh axis runs over, the one named last changes fastest.
Arguments:
- vectors: float32 [32768, 2048], P('row', 'vec'), may hold values from -6 to 6
- reflectors: float32 [3, 32768, 512], P(None, ('row', 'vec')), may hold values from -0.03125 to 0.03125
- triangles: float32 [3, 512, 512], P(None, None, 'vec'), may hold values from -0.04 to 2, as said below
Outputs:
- transformed: float32 [32768, 2048], P('row', 'vec')
Inputs may be any that keep to these rules, and one draw needn't show every extreme that they name: Each triangles[k] is upper triangular with a diagonal between 0.5 and 2.
All inputs are finite; a program needn't handle non-finite values.
Results may differ from a plain program's by a relative error of at most 0.0001.
Values sent between devices are 32-bit elements; how exact they have to be, the bound alone decides.
A program may use at most 64 MiB of HBM per device.

v0:
```python
import jax
import jax.numpy as jnp
from jax import lax
from jax.sharding import Mesh
from jax.sharding import PartitionSpec as P

VEC = ("vec_0", "vec_1")
ROW_VEC = ("row", "vec_0", "vec_1")


def whole_of(x, axes, dim):
    for axis in reversed(axes):
        x = lax.all_gather(x, axis, axis=dim, tiled=True)
    return x


def cut_along(x, dim, count):
    before, after = (x.shape[:dim], x.shape[dim + 1 :])
    return jnp.moveaxis(x.reshape(*before, count, -1, *after), dim, 0)


def summed_on_arrival(x, axis, dim):
    count = lax.axis_size(axis)
    blocks = lax.all_to_all(cut_along(x, dim, count), axis, 0, 0, tiled=True)
    return jnp.sum(blocks, axis=0)


def from_everyone(x, axis):
    count = lax.axis_size(axis)
    return lax.all_to_all(jnp.broadcast_to(x[None], (count, *x.shape)), axis, 0, 0, tiled=True)


def laid_out(blocks, dim):
    lengths = list(blocks.shape[1:])
    lengths[dim] *= blocks.shape[0]
    return jnp.moveaxis(blocks, 0, dim).reshape(lengths)


def collect(x, axis, dim):
    blocks = from_everyone(x, axis)
    return laid_out(blocks, dim)


def per_device(vectors, reflectors, triangles):
    highest = lax.Precision.HIGHEST
    panels = reflectors.shape[0]
    current = vectors
    sections = lax.all_gather(reflectors, VEC, axis=1, tiled=True)
    factors = whole_of(triangles, VEC, 2)
    for step in range(panels):
        panel = panels - 1 - step
        section = sections[panel]
        factor = factors[panel]
        partial_value = lax.dot_general(
            section,
            current,
            (((0,), (0,)), ((), ())),
            precision=highest,
            preferred_element_type=jnp.float32,
        )
        share = summed_on_arrival(partial_value, "row", 1)
        owned = jnp.dot(factor, share, precision=highest, preferred_element_type=jnp.float32)
        coefficients = collect(owned, "row", 1)
        current = current - jnp.dot(
            section, coefficients, precision=highest, preferred_element_type=jnp.float32
        )
    return current


def solution(mesh):
    finer = Mesh(mesh.devices.reshape(mesh.shape["row"], 4, 4), ("row", "vec_0", "vec_1"))
    placed = (P("row", VEC), P(None, ROW_VEC, None), P(None, None, VEC))
    return jax.shard_map(
        per_device, mesh=finer, in_specs=placed, out_specs=P("row", VEC), check_vma=False
    )
```

profile of v0, /device:TPU:1, one launch (start us, length us, event | category | flops | bytes accessed | tf_op | source)
XLA Modules:
  0.0 311.0 jit_solution(14054268650420613728)
XLA Ops:
  6.5 0.7 all-gather.3.cloned.1.call-update
  7.3 14.0 %all_gather.10 = f32[3,512,128]{1,2,0:T(8,128)} all-gather(f32[3,512,32]{1,2,0:T(8,128)} %param.5), channel_id=1, replica_groups=mesh['row'=32,'vec_0'=4,'vec_1'=4] {'vec_1'}, dimensions={2}, use_global_device_ids=true | all-gather | bytes 983040 | tf_op jit(solution)/shard_map/all_gather | solution.py:13
  21.3 1.2 copy.17
  22.6 0.1 dot_general.48
  22.7 69.4 %all-gather.3.cloned.1.call-done = f32[3,1024,512]{2,1,0:T(8,128)} async-done(((f32[3,64,512]{2,1,0:T(8,128)}), f32[3,1024,512]{2,1,0:T(8,128)}) %all-gather.3.cloned.1.call-update) | async-done | bytes 6291472 | tf_op jit(solution)/shard_map/all_gather | solution.py:48
  92.1 3.1 fusion.22
  95.2 0.2 copy.19
  95.4 35.2 %all_to_all.30 = f32[32,512,4]{1,2,0:T(4,128)S(1)} all-to-all(f32[32,512,4]{1,2,0:T(4,128)S(1)} %copy.19), channel_id=1, replica_groups=mesh['row'=32,'vec_0'=4,'vec_1'=4] {'row'}, dimensions={0} | all-to-all | bytes 524288 | tf_op jit(solution)/shard_map/all_to_all | solution.py:24
  130.6 0.1 reduce_sum.27
  130.7 10.5 %all-gather.5.cloned.1.call-done = f32[3,512,512]{1,2,0:T(8,128)} async-done(((f32[3,512,128]{1,2,0:T(8,128)}), f32[3,512,512]{1,2,0:T(8,128)}) %all-gather.5.cloned.1.call-update) | async-done | bytes 3145744 | tf_op jit(solution)/shard_map/all_gather | solution.py:13
  141.2 1.8 convolution_bitcast_fusion.2
  143.0 0.7 broadcast_in_dim.6
  143.8 13.2 %all-to-all-start.1 = ((f32[32,512,4]{1,2,0:T(4,128)}), f32[32,512,4]{1,2,0:T(4,128)S(1)}, u32[]{:S(2)}, u32[]{:S(2)}) async-start(f32[32,512,4]{1,2,0:T(4,128)} %broadcast_in_dim.6), calls=%async_computation.1 | async-start | bytes 524288 | tf_op jit(solution)/shard_map/all_to_all | solution.py:30
  157.0 0.2 copy.20
  157.2 22.0 %all-to-all-done.1 = f32[32,512,4]{1,2,0:T(4,128)S(1)} async-done(((f32[32,512,4]{1,2,0:T(4,128)}), f32[32,512,4]{1,2,0:T(4,128)S(1)}, u32[]{:S(2)}, u32[]{:S(2)}) %all-to-all-start.1) | async-done | bytes 262176 | tf_op jit(solution)/shard_map/all_to_all | solution.py:30
  179.2 0.1 reshape.20
  179.3 3.9 %fusion.15 = f32[1024,128]{0,1:T(8,128)S(1)} fusion(f32[1024,128]{0,1:T(8,128)S(1)} %copy.20, f32[512,128]{0,1:T(8,128)S(1)} %reshape.20, f32[3,1024,512]{2,1,0:T(8,128)} %all-gather.3.cloned.1.call-done), kind=kOutput, calls=%fused_computation.15 | convolution fusion | flops 805437440 | bytes 3407872 | tf_op jit(solution)/shard_map/dot_general | solution.py:64
  183.2 2.9 fusion.21
  186.1 0.1 reshape.21
  186.1 24.9 %all_to_all.31 = f32[32,512,4]{1,2,0:T(4,128)S(1)} all-to-all(f32[32,512,4]{1,2,0:T(4,128)S(1)} %bitcast.91), channel_id=1, replica_groups=mesh['row'=32,'vec_0'=4,'vec_1'=4] {'row'}, dimensions={0} | all-to-all | bytes 524288 | tf_op jit(solution)/shard_map/all_to_all | solution.py:24
  211.1 1.8 convolution_bitcast_fusion.1
  213.0 25.9 %all_to_all.32 = f32[32,512,4]{1,2,0:T(4,128)S(1)} all-to-all(f32[32,512,4]{1,2,0:T(4,128)S(1)} %broadcast_in_dim.7), channel_id=1, replica_groups=mesh['row'=32,'vec_0'=4,'vec_1'=4] {'row'}, dimensions={0} | all-to-all | bytes 524288 | tf_op jit(solution)/shard_map/all_to_all | solution.py:30
  238.9 0.1 reshape.22
  239.0 3.9 %fusion.18 = f32[1024,128]{0,1:T(8,128)S(1)} fusion(f32[1024,128]{0,1:T(8,128)S(1)} %fusion.15, f32[512,128]{0,1:T(8,128)S(1)} %reshape.22, f32[3,1024,512]{2,1,0:T(8,128)} %all-gather.3.cloned.1.call-done), kind=kOutput, calls=%fused_computation.16 | convolution fusion | flops 805437440 | bytes 3407872 | tf_op jit(solution)/shard_map/dot_general | solution.py:64
  242.9 2.9 fusion.20
  245.8 0.1 reshape.23
  245.8 25.6 %all_to_all.33 = f32[32,512,4]{1,2,0:T(4,128)S(1)} all-to-all(f32[32,512,4]{1,2,0:T(4,128)S(1)} %bitcast.93), channel_id=1, replica_groups=mesh['row'=32,'vec_0'=4,'vec_1'=4] {'row'}, dimensions={0} | all-to-all | bytes 524288 | tf_op jit(solution)/shard_map/all_to_all | solution.py:24
  271.5 1.8 convolution_bitcast_fusion
  273.4 25.8 %all_to_all.34 = f32[32,512,4]{1,2,0:T(4,128)S(1)} all-to-all(f32[32,512,4]{1,2,0:T(4,128)S(1)} %broadcast_in_dim.8), channel_id=1, replica_groups=mesh['row'=32,'vec_0'=4,'vec_1'=4] {'row'}, dimensions={0} | all-to-all | bytes 524288 | tf_op jit(solution)/shard_map/all_to_all | solution.py:30
  299.2 0.1 reshape.24
  299.3 3.9 %fusion.19 = f32[1024,128]{0,1:T(8,128)S(1)} fusion(f32[1024,128]{0,1:T(8,128)S(1)} %fusion.18, f32[512,128]{0,1:T(8,128)S(1)} %reshape.24, f32[3,1024,512]{2,1,0:T(8,128)} %all-gather.3.cloned.1.call-done), kind=kOutput, calls=%fused_computation.17 | convolution fusion | flops 805437440 | bytes 3407872 | tf_op jit(solution)/shard_map/dot_general | solution.py:64
  303.1 1.0 copy.21
  (9 shorter events, 0.3 us)
Async XLA Ops:
  6.5 85.6 %all-gather.3.cloned.1.call-start = ((), (), s32[]{:S(2)}) async-start(), calls=%async_computation.6 | async-start | bytes 6684672 | tf_op jit(solution)/shard_map/all_gather | solution.py:48
  7.3 133.9 %all-gather.5.cloned.1.call-start = ((), (), s32[]{:S(2)}) async-start(), calls=%async_computation.7 | async-start | bytes 3932160 | tf_op jit(solution)/shard_map/all_gather | solution.py:13
  22.7 134.2 %copy-start = (f32[1024,128]{1,0:T(8,128)S(1)}, f32[1024,128]{1,0:T(8,128)}, u32[]{:S(2)}) copy-start(f32[1024,128]{1,0:T(8,128)} %param.3) | copy-start | bytes 1572868
  143.8 35.4 %all-to-all-start.1 = ((f32[32,512,4]{1,2,0:T(4,128)}), f32[32,512,4]{1,2,0:T(4,128)S(1)}, u32[]{:S(2)}, u32[]{:S(2)}) async-start(f32[32,512,4]{1,2,0:T(4,128)} %broadcast_in_dim.6), calls=%async_computation.1 | async-start | bytes 524288 | tf_op jit(solution)/shard_map/all_to_all | solution.py:30
Sparse Core Ops, SparseCore 0:
  10.3 81.6 all-gather.2
  94.2 46.9 all-gather.4
where the time goes:
time: 312 us; the launch traced here: 311 us
  blocking collectives  151 us (48%)
  waiting for transfers between devices  103 us (33%)
  matrix products  25.9 us (8%)
  between operations  13.5 us (4%)
  starting transfers between devices  13.2 us (4%)
  local copies, waits for them, and re-layouts  3.99 us (1%)
    all_to_all x3, blocking collectives, summed_on_arrival(): blocks = lax.all_to_all(cut_along(x, dim, count), axis, 0, 0, tiled=True)  85.8 us
    all_gather x1, waiting for transfers between devices, per_device(): sections = lax.all_gather(reflectors, VEC, axis=1, tiled=True)  69.4 us
    all_to_all x2, blocking collectives, from_everyone(): lax.all_to_all(jnp.broadcast_to(x[None], (count, *x.shape)), axis, 0, 0,...  51.7 us
    all_to_all x1, waiting for transfers between devices, from_everyone(): lax.all_to_all(jnp.broadcast_to(x[None], (count, *x.shape)), axis, 0, 0,...  22 us
    all_gather x1, blocking collectives, whole_of(): x = lax.all_gather(x, axis, axis=dim, tiled=True)  14 us
    all_to_all x1, starting transfers between devices, from_everyone(): lax.all_to_all(jnp.broadcast_to(x[None], (count, *x.shape)), axis, 0, 0,...  13.2 us
    dot_general x3, matrix products, per_device(): jnp.dot(section, coefficients, precision=highest, preferred_element_type=...  11.6 us
    all_gather x1, waiting for transfers between devices, whole_of(): x = lax.all_gather(x, axis, axis=dim, tiled=True)  10.5 us
  transfers between devices with their start and end apart: 3, of which 3 were waited for; matrix products, arithmetic and copies ran while one was open for 2% of the time, Pallas kernels for 0%

commit v1 on v0

--- a/solution.py
+++ b/solution.py
@@ -3,9 +3,16 @@
 from jax import lax
 from jax.sharding import Mesh
 from jax.sharding import PartitionSpec as P
+from jax.lax import all_to_all, psum
 
 VEC = ("vec_0", "vec_1")
 ROW_VEC = ("row", "vec_0", "vec_1")
+
+
+def raise_table_for(shard_in):
+    return jnp.concatenate(
+        all_to_all(jnp.stack([shard_in for _ in range(psum(1, VEC))], axis=0), VEC, 0, 0), 1
+    )
 
 
 def whole_of(x, axes, dim):
@@ -45,7 +52,7 @@
     highest = lax.Precision.HIGHEST
     panels = reflectors.shape[0]
     current = vectors
-    sections = lax.all_gather(reflectors, VEC, axis=1, tiled=True)
+    sections = raise_table_for(reflectors)
     factors = whole_of(triangles, VEC, 2)
     for step in range(panels):
         panel = panels - 1 - step

time: 312 us -> 338 us (1.083)
  blocking collectives: 151 us -> 243 us
  waiting for transfers between devices: 103 us -> 24.5 us
  local copies, waits for them, and re-layouts: 3.99 us -> 14.8 us
  starting transfers between devices: 13.2 us -> 21 us
  matrix products: 25.9 us -> 19.8 us
    all_gather x1, blocking collectives: 14 us -> 94.2 us  [whole_of(): x = lax.all_gather(x, axis, axis=dim, tiled=True)]
    all_gather x1 -> x0, waiting for transfers between devices: 69.4 us -> none  [per_device(): sections = lax.all_gather(reflectors, VEC, axis=1, tiled=True)]
    all_to_all x3, blocking collectives: 85.8 us -> 97.5 us  [summed_on_arrival(): blocks = lax.all_to_all(cut_along(x, dim, count), axis, 0, 0, tiled=True)]
    all_to_all x0 -> x1, starting transfers between devices: none -> 7.75 us  [raise_table_for(): all_to_all(jnp.stack([shard_in for _ in range(psum(1, VEC))], axis=0), VE...]
    all_gather x1, waiting for transfers between devices: 10.5 us -> 3.17 us  [whole_of(): x = lax.all_gather(x, axis, axis=dim, tiled=True)]
    slice x0 -> x1, local copies, waits for them, and re-layouts: none -> 5.25 us  [per_device(): section = sections[panel]]
    dot_general x3, matrix products: 8.86 us -> 4.12 us  [per_device(): lax.dot_general(section, current, (((0,), (0,)), ((), ())), precision=hig...]
    another operation x0 -> x1, local copies, waits for them, and re-layouts: none -> 4.45 us  [raise_table_for(): jnp.stack([shard_in for _ in range(psum(1, VEC))], axis=0)]
  transfers between devices with their start and end apart: 3 -> 3, of which waited for: 3 -> 2; matrix products, arithmetic and copies ran while one was open for 2% -> 2% of each run, Pallas kernels for 0% -> 0%
where the time goes in v1:
time: 338 us; the launch traced here: 337 us
  blocking collectives  243 us (72%)
  waiting for transfers between devices  24.5 us (7%)
  starting transfers between devices  21 us (6%)
  matrix products  19.8 us (6%)
  local copies, waits for them, and re-layouts  14.8 us (4%)
  between operations  13.6 us (4%)
    all_to_all x3, blocking collectives, summed_on_arrival(): blocks = lax.all_to_all(cut_along(x, dim, count), axis, 0, 0, tiled=True)  97.5 us
    all_gather x1, blocking collectives, whole_of(): x = lax.all_gather(x, axis, axis=dim, tiled=True)  94.2 us
    all_to_all x2, blocking collectives, from_everyone(): lax.all_to_all(jnp.broadcast_to(x[None], (count, *x.shape)), axis, 0, 0,...  51.7 us
    all_to_all x1, waiting for transfers between devices, from_everyone(): lax.all_to_all(jnp.broadcast_to(x[None], (count, *x.shape)), axis, 0, 0,...  21.3 us
    all_to_all x1, starting transfers between devices, from_everyone(): lax.all_to_all(jnp.broadcast_to(x[None], (count, *x.shape)), axis, 0, 0,...  13.2 us
    dot_general x3, matrix products, per_device(): jnp.dot(section, coefficients, precision=highest, preferred_element_type=...  10.2 us
    all_to_all x1, starting transfers between devices, raise_table_for(): all_to_all(jnp.stack([shard_in for _ in range(psum(1, VEC))], axis=0), VE...  7.75 us
  transfers between devices with their start and end apart: 3, of which 2 were waited for; matrix products, arithmetic and copies ran while one was open for 2% of the time, Pallas kernels for 0%

profile of v1, /device:TPU:1, one launch (start us, length us, event | category | flops | bytes accessed | tf_op | source)
XLA Modules:
  0.0 337.3 jit_solution(9733743806230166137)
XLA Ops:
  6.5 4.5 %stack.2 = f32[16,3,64,512]{3,2,1,0:T(8,128)} broadcast(f32[3,64,512]{2,1,0:T(8,128)} %param.4), dimensions={1,2,3} | broadcast | bytes 6684672 | tf_op jit(solution)/shard_map/stack | solution.py:14
  11.0 7.7 %all-to-all-start = ((f32[16,3,64,512]{3,2,1,0:T(8,128)}), f32[16,3,64,512]{3,2,1,0:T(8,128)}, u32[]{:S(2)}, u32[]{:S(2)}) async-start(f32[16,3,64,512]{3,2,1,0:T(8,128)} %stack.2), calls=%async_computation | async-start | bytes 12582912 | tf_op jit(solution)/shard_map/all_to_all | solution.py:14
  18.8 94.2 %all_gather.6 = f32[3,512,128]{1,2,0:T(8,128)} all-gather(f32[3,512,32]{1,2,0:T(8,128)S(1)} %copy-done.3), channel_id=1, replica_groups=mesh['row'=32,'vec_0'=4,'vec_1'=4] {'vec_1'}, dimensions={2}, use_global_device_ids=true | all-gather | bytes 983040 | tf_op jit(solution)/shard_map/all_gather | solution.py:20
  113.1 0.2 copy.17
  113.3 0.1 dot_general.48
  113.5 5.3 %fusion.4 = (f32[1,16,64,512]{3,2,0,1:T(8,128)S(1)}, f32[1,16,64,512]{3,2,0,1:T(8,128)}, f32[1,16,64,512]{3,2,0,1:T(8,128)S(1)}) fusion(f32[3,16,64,512]{3,2,0,1:T(8,128)} %bitcast), kind=kLoop, calls=%fused_computation.16 | loop fusion | bytes 12582912 | tf_op jit(solution)/shard_map/slice | solution.py:59
  118.7 1.4 copy-done.1
  120.1 1.5 convolution_bitcast_fusion.5
  121.6 0.2 copy.19
  121.8 47.0 %all_to_all.35 = f32[32,512,4]{1,2,0:T(4,128)S(1)} all-to-all(f32[32,512,4]{1,2,0:T(4,128)S(1)} %copy.19), channel_id=1, replica_groups=mesh['row'=32,'vec_0'=4,'vec_1'=4] {'row'}, dimensions={0} | all-to-all | bytes 524288 | tf_op jit(solution)/shard_map/all_to_all | solution.py:31
  168.8 3.2 all-gather.2.cloned.1.call-done
  172.0 1.8 convolution_bitcast_fusion.8
  173.8 0.7 broadcast_in_dim.6
  174.6 13.2 %all-to-all-start.2 = ((f32[32,512,4]{1,2,0:T(4,128)}), f32[32,512,4]{1,2,0:T(4,128)S(1)}, u32[]{:S(2)}, u32[]{:S(2)}) async-start(f32[32,512,4]{1,2,0:T(4,128)} %broadcast_in_dim.6), calls=%async_computation.2 | async-start | bytes 524288 | tf_op jit(solution)/shard_map/all_to_all | solution.py:37
  187.8 1.0 copy.20
  188.8 21.3 %all-to-all-done.2 = f32[32,512,4]{1,2,0:T(4,128)S(1)} async-done(((f32[32,512,4]{1,2,0:T(4,128)}), f32[32,512,4]{1,2,0:T(4,128)S(1)}, u32[]{:S(2)}, u32[]{:S(2)}) %all-to-all-start.2) | async-done | bytes 262176 | tf_op jit(solution)/shard_map/all_to_all | solution.py:37
  210.0 0.1 reshape.33
  210.1 4.1 %fusion = f32[1024,128]{0,1:T(8,128)S(1)} fusion(f32[1024,128]{0,1:T(8,128)} %copy.20, f32[512,128]{0,1:T(8,128)S(1)} %reshape.33, f32[1024,512]{1,0:T(8,128)} %bitcast.74), kind=kOutput, calls=%fused_computation.3 | convolution fusion | flops 805437440 | bytes 3407872 | tf_op jit(solution)/shard_map/dot_general | solution.py:71
  214.2 1.3 convolution_bitcast_fusion.4
  215.5 0.1 reshape.34
  215.6 24.9 %all_to_all.36 = f32[32,512,4]{1,2,0:T(4,128)S(1)} all-to-all(f32[32,512,4]{1,2,0:T(4,128)S(1)} %bitcast.77), channel_id=1, replica_groups=mesh['row'=32,'vec_0'=4,'vec_1'=4] {'row'}, dimensions={0} | all-to-all | bytes 524288 | tf_op jit(solution)/shard_map/all_to_all | solution.py:31
  240.6 1.8 convolution_bitcast_fusion.7
  242.5 25.9 %all_to_all.37 = f32[32,512,4]{1,2,0:T(4,128)S(1)} all-to-all(f32[32,512,4]{1,2,0:T(4,128)S(1)} %broadcast_in_dim.7), channel_id=1, replica_groups=mesh['row'=32,'vec_0'=4,'vec_1'=4] {'row'}, dimensions={0} | all-to-all | bytes 524288 | tf_op jit(solution)/shard_map/all_to_all | solution.py:37
  268.4 0.1 reshape.35
  268.5 3.9 %fusion.1 = f32[1024,128]{0,1:T(8,128)S(1)} fusion(f32[1024,128]{0,1:T(8,128)S(1)} %fusion, f32[512,128]{0,1:T(8,128)S(1)} %reshape.35, f32[1024,512]{1,0:T(8,128)} %bitcast.71), kind=kOutput, calls=%fused_computation.4 | convolution fusion | flops 805437440 | bytes 3407872 | tf_op jit(solution)/shard_map/dot_general | solution.py:71
  272.3 1.3 convolution_bitcast_fusion.3
  273.7 25.6 %all_to_all.38 = f32[32,512,4]{1,2,0:T(4,128)S(1)} all-to-all(f32[32,512,4]{1,2,0:T(4,128)S(1)} %bitcast.79), channel_id=1, replica_groups=mesh['row'=32,'vec_0'=4,'vec_1'=4] {'row'}, dimensions={0} | all-to-all | bytes 524288 | tf_op jit(solution)/shard_map/all_to_all | solution.py:31
  299.4 1.8 convolution_bitcast_fusion.6
  301.3 25.8 %all_to_all.39 = f32[32,512,4]{1,2,0:T(4,128)S(1)} all-to-all(f32[32,512,4]{1,2,0:T(4,128)S(1)} %broadcast_in_dim.8), channel_id=1, replica_groups=mesh['row'=32,'vec_0'=4,'vec_1'=4] {'row'}, dimensions={0} | all-to-all | bytes 524288 | tf_op jit(solution)/shard_map/all_to_all | solution.py:37
  327.0 0.1 reshape.37
  327.1 2.3 fusion.2
  329.4 1.0 copy.21
  (16 shorter events, 0.4 us)
Async XLA Ops:
  11.0 7.8 %copy-start.3 = (f32[3,512,32]{1,2,0:T(8,128)S(1)}, f32[3,512,32]{1,2,0:T(8,128)}, u32[]{:S(2)}) copy-start(f32[3,512,32]{1,2,0:T(8,128)} %param.5) | copy-start | bytes 589828
  11.0 102.5 %all-to-all-start = ((f32[16,3,64,512]{3,2,1,0:T(8,128)}), f32[16,3,64,512]{3,2,1,0:T(8,128)}, u32[]{:S(2)}, u32[]{:S(2)}) async-start(f32[16,3,64,512]{3,2,1,0:T(8,128)} %stack.2), calls=%async_computation | async-start | bytes 12582912 | tf_op jit(solution)/shard_map/all_to_all | solution.py:14
  18.7 94.3 %copy-start.2 = (f32[1024,128]{1,0:T(8,128)S(1)}, f32[1024,128]{1,0:T(8,128)}, u32[]{:S(2)}) copy-start(f32[1024,128]{1,0:T(8,128)} %param.3) | copy-start | bytes 1572868
  18.8 153.2 %all-gather.2.cloned.1.call-start = ((), (), s32[]{:S(2)}) async-start(), calls=%async_computation.7 | async-start | bytes 3932160 | tf_op jit(solution)/shard_map/all_gather | solution.py:20
  118.7 1.4 copy-start.1
  174.6 35.4 %all-to-all-start.2 = ((f32[32,512,4]{1,2,0:T(4,128)}), f32[32,512,4]{1,2,0:T(4,128)S(1)}, u32[]{:S(2)}, u32[]{:S(2)}) async-start(f32[32,512,4]{1,2,0:T(4,128)} %broadcast_in_dim.6), calls=%async_computation.2 | async-start | bytes 524288 | tf_op jit(solution)/shard_map/all_to_all | solution.py:37
  210.1 4.1 %copy-start = (f32[1,16,64,512]{3,2,0,1:T(8,128)S(1)}, f32[1,16,64,512]{3,2,0,1:T(8,128)}, u32[]{:S(2)}) copy-start(f32[1,16,64,512]{3,2,0,1:T(8,128)} %get-tuple-element.6) | copy-start | bytes 6291460
Sparse Core Ops, SparseCore 0:
  113.2 58.7 all-gather.1
